TPU v7x, 256 devices: a whole 4x4x8 slice. The times are simulated.
256 devices in a mesh: batch: 64 (over z, y, core), group: 4 (over x).
Axes of the slice: x: 4, y: 4, z: 8, core: 2. Of those that a mesh axis runs over, the one named last changes fastest.
Arguments:
- samples_in: float32 [16384, 8192], P('batch', 'group'), may hold values from -8 to 8, as said below
- second_samples_in: float32 [16384, 8192], P('batch', 'group'), may hold values from -8 to 8, as said below
Outputs:
- standard: float32 [16384, 8192], P(None, ('group', 'batch'))
- second_standard: float32 [16384, 8192], P(None, ('group', 'batch'))
Inputs may be any that keep to these rules, and one draw needn't show every extreme that they name: samples_in holds numbers from -8 to 8. second_samples_in holds numbers from -8 to 8.
All inputs are finite; a program needn't handle non-finite values.
Results may differ from a plain program's by a relative error of at most 0.0003.
Values sent between devices are 32-bit elements.
A program may use at most 64 MiB of HBM per device.

v0:
```python
import jax
import jax.numpy as jnp
from jax import lax
from jax.sharding import PartitionSpec as P


def shards(samples_in, second_samples_in):
    moved_samples_in, moved_second_samples_in = (
        lax.all_to_all(samples_in, "batch", split_axis=1, concat_axis=0, tiled=True),
        lax.all_to_all(second_samples_in, "batch", split_axis=1, concat_axis=0, tiled=True),
    )
    wide_standard = moved_samples_in.astype(jnp.float32)
    low_standard = jnp.mean(jnp.minimum(wide_standard, 1.0), axis=0)
    high_standard = jnp.mean(jnp.maximum(wide_standard, 1.0), axis=0)
    standard = (wide_standard - low_standard) / (high_standard - low_standard + 0.1)
    wide_second_standard = moved_second_samples_in.astype(jnp.float32)
    low_second_standard = jnp.mean(jnp.minimum(wide_second_standard, 1.0), axis=0)
    high_second_standard = jnp.mean(jnp.maximum(wide_second_standard, 1.0), axis=0)
    second_standard = (wide_second_standard - low_second_standard) / (
        high_second_standard - low_second_standard + 0.1
    )
    return (standard, second_standard)


def solution(mesh):
    placed = (P("batch", "group"), P("batch", "group"))
    return jax.shard_map(
        shards,
        mesh=mesh,
        in_specs=placed,
        out_specs=(P(None, ("group", "batch")), P(None, ("group", "batch"))),
        check_vma=False,
    )
```

profile of v0, /device:TPU:1, one launch (start us, length us, event | category | flops | bytes accessed | tf_op | source)
XLA Modules:
  0.0 131.2 jit_solution(1212408912967715892)
XLA Ops:
  0.6 2.9 %copy.8 = f32[256,2048]{0,1:T(8,128)} copy(f32[256,2048]{1,0:T(8,128)} %param.2) | data formatting | bytes 4194304 | tf_op args[0]
  3.5 13.2 %all-to-all-start = ((f32[256,64,32]{0,2,1:T(8,128)}), f32[256,64,32]{0,2,1:T(8,128)S(1)}, u32[]{:S(2)}, u32[]{:S(2)}) async-start(f32[256,64,32]{0,2,1:T(8,128)} %bitcast.24), calls=%async_computation | async-start | bytes 4194304 | tf_op jit(solution)/shard_map/all_to_all | solution.py:9
  16.7 2.9 %copy.10 = f32[256,2048]{0,1:T(8,128)} copy(f32[256,2048]{1,0:T(8,128)} %param.3) | data formatting | bytes 4194304 | tf_op args[1]
  19.6 47.1 %all-to-all-done = f32[256,64,32]{0,2,1:T(8,128)S(1)} async-done(((f32[256,64,32]{0,2,1:T(8,128)}), f32[256,64,32]{0,2,1:T(8,128)S(1)}, u32[]{:S(2)}, u32[]{:S(2)}) %all-to-all-start) | async-done | bytes 2097184 | tf_op jit(solution)/shard_map/all_to_all | solution.py:9
  66.6 7.4 %all-to-all-start.1 = ((f32[256,64,32]{0,2,1:T(8,128)}), f32[256,64,32]{0,2,1:T(8,128)}, u32[]{:S(2)}, u32[]{:S(2)}) async-start(f32[256,64,32]{0,2,1:T(8,128)} %bitcast.23), calls=%async_computation.1 | async-start | bytes 4194304 | tf_op jit(solution)/shard_map/all_to_all | solution.py:10
  74.1 1.5 %copy.12 = f32[64,4,8,256]{3,2,0,1:T(8,128)} copy(f32[64,4,8,256]{3,2,1,0:T(8,128)S(1)} %bitcast.20) | data formatting | bytes 4194304 | tf_op jit(solution)/shard_map/all_to_all | solution.py:9
  75.6 48.7 %all-to-all-done.1 = f32[256,64,32]{0,2,1:T(8,128)} async-done(((f32[256,64,32]{0,2,1:T(8,128)}), f32[256,64,32]{0,2,1:T(8,128)}, u32[]{:S(2)}, u32[]{:S(2)}) %all-to-all-start.1) | async-done | bytes 2097184 | tf_op jit(solution)/shard_map/all_to_all | solution.py:10
  124.2 1.8 %copy.13 = f32[64,4,8,256]{3,2,0,1:T(8,128)S(1)} copy(f32[64,4,8,256]{3,2,1,0:T(8,128)} %bitcast.6) | data formatting | bytes 4194304 | tf_op jit(solution)/shard_map/all_to_all | solution.py:10
  126.0 0.0 copy-start
  126.0 0.5 fusion.3
  126.5 2.1 %fusion.1 = (f32[32]{0:T(128)S(1)}, f32[32]{0:T(128)S(1)}) fusion(f32[256,64,32]{0,2,1:T(8,128)} %all-to-all-done.1), kind=kLoop, calls=%fused_computation.3 | loop fusion | flops 2097088 | bytes 2097408 | tf_op jit(solution)/shard_map/reduce_sum | solution.py:17
  128.7 0.0 copy-done
  128.7 2.5 %subtract_divide_fusion = (f32[16384,32]{0,1:T(8,128)}, f32[16384,32]{0,1:T(8,128)}) fusion(f32[16384,32]{0,1:T(8,128)S(1)} %bitcast.22, f32[32]{0:T(128)S(1)} %get-tuple-element.7, f32[32]{0:T(128)S(1)} %get-tuple-element.6, f32[32]{0:T(128)S(1)} %get-tuple-element.9, f32[16384,32]{0,1:T(8,128)S(1)} %bitcast.21, f32[32]{0:T(128)S(1)} %get-tuple-element.8), kind=kLoop, calls=%fused_computation.8 | loop fusion | flops 2097152 | bytes 8389120 | tf_op jit(solution)/shard_map/div | solution.py:19
  (2 shorter events, 0.0 us)
Async XLA Ops:
  3.5 63.1 %all-to-all-start = ((f32[256,64,32]{0,2,1:T(8,128)}), f32[256,64,32]{0,2,1:T(8,128)S(1)}, u32[]{:S(2)}, u32[]{:S(2)}) async-start(f32[256,64,32]{0,2,1:T(8,128)} %bitcast.24), calls=%async_computation | async-start | bytes 4194304 | tf_op jit(solution)/shard_map/all_to_all | solution.py:9
  66.6 57.6 %all-to-all-start.1 = ((f32[256,64,32]{0,2,1:T(8,128)}), f32[256,64,32]{0,2,1:T(8,128)}, u32[]{:S(2)}, u32[]{:S(2)}) async-start(f32[256,64,32]{0,2,1:T(8,128)} %bitcast.23), calls=%async_computation.1 | async-start | bytes 4194304 | tf_op jit(solution)/shard_map/all_to_all | solution.py:10
  126.0 2.6 %copy-start = (f32[64,4,8,256]{3,2,0,1:T(8,128)S(1)}, f32[64,4,8,256]{3,2,0,1:T(8,128)}, u32[]{:S(2)}) copy-start(f32[64,4,8,256]{3,2,0,1:T(8,128)} %copy.12) | copy-start | bytes 6291460
where the time goes:
time: 132 us; the launch traced here: 131 us
  waiting for transfers between devices  95.7 us (72%)
  starting transfers between devices  20.6 us (16%)
  local copies, waits for them, and re-layouts  9.08 us (7%)
  other arithmetic  5.11 us (4%)
    all_to_all x1, waiting for transfers between devices, shards(): lax.all_to_all(second_samples_in, 'batch', split_axis=1, concat_axis=0, t...  48.7 us
    all_to_all x1, waiting for transfers between devices, shards(): lax.all_to_all(samples_in, 'batch', split_axis=1, concat_axis=0, tiled=True)  47.1 us
    all_to_all x1, starting transfers between devices, shards(): lax.all_to_all(samples_in, 'batch', split_axis=1, concat_axis=0, tiled=True)  13.2 us
    all_to_all x1, starting transfers between devices, shards(): lax.all_to_all(second_samples_in, 'batch', split_axis=1, concat_axis=0, t...  7.41 us
    unnamed x4, local copies, waits for them, and re-layouts  5.78 us
  transfers between devices with their start and end apart: 2, of which 2 were waited for; matrix products, arithmetic and copies ran while one was open for 3% of the time, Pallas kernels for 0%

commit v1 on v0

v1 whole, which is shorter than its diff:
```python
import jax
import jax.numpy as jnp
from jax import lax
from jax.experimental import pallas as pl
from jax.experimental.pallas import tpu as pltpu
from jax.sharding import PartitionSpec as P

MESH = pl.DeviceIdType.MESH
N = 64
ROWS, WIDE, NARROW = 256, 2048, 32
STEPS = (1, 7, 2, 6, 3, 5, 4, 0)


def device(me, dz, across):
    z, y, c = me // 8, (me // 2) % 4, me % 2
    return ((z + dz) % 8) * 8 + ((y + across % 4) % 4) * 2 + (c + across // 4) % 2


def kernel(a_ref, b_ref, first_out, second_out, held, turned, landed, in_sem, send_sem, recv_sem):
    me = lax.axis_index("batch")
    z = me // 8

    def load(which, step):
        columns = pl.ds(pl.multiple_of(((z + STEPS[step]) % 8) * ROWS, ROWS), ROWS)
        source = (a_ref, b_ref)[which]
        return pltpu.make_async_copy(
            source.at[:, columns], held.at[which, :, columns], in_sem.at[which, step]
        )

    for step in range(8):
        for which in range(2):
            load(which, step).start()

    barrier = pltpu.get_barrier_semaphore()

    def greet(i, carry):
        pl.semaphore_signal(
            barrier, inc=1, device_id={"batch": (me + i) % N}, device_id_type=MESH
        )
        return carry

    lax.fori_loop(1, N, greet, 0)

    def turn(step):
        zt = (z + STEPS[step]) % 8
        columns = pl.ds(pl.multiple_of(zt * ROWS, ROWS), ROWS)
        for which in range(2):
            load(which, step).wait()
            block = held[which, :, columns].T
            turned[pl.ds(zt * 8, 8), which * NARROW : (which + 1) * NARROW, :] = block.reshape(
                8, NARROW, ROWS
            )

    def send(round_, step):
        to = device(me, STEPS[step], (step + round_) % 8)
        pltpu.make_async_remote_copy(
            src_ref=turned.at[to],
            dst_ref=landed.at[me],
            send_sem=send_sem,
            recv_sem=recv_sem.at[round_],
            device_id={"batch": to},
            device_id_type=MESH,
        ).start()

    turn(0)
    pl.semaphore_wait(barrier, N - 1)
    for step in range(1, 8):
        turn(step)
        send(0, step - 1)
    send(0, 7)

    def send_round(round_, carry):
        for step in range(7):
            send(round_, step)

        @pl.when(round_ != 1)
        def _():
            send(round_, 7)

        return carry

    lax.fori_loop(1, 8, send_round, 0)

    def add(block, sums):
        low, high = sums
        left, right = block[:, :128], block[:, 128:]
        low = low + (jnp.minimum(left, 1.0) + jnp.minimum(right, 1.0))
        high = high + (jnp.maximum(left, 1.0) + jnp.maximum(right, 1.0))
        return low, high

    landed[me] = turned[me]
    sums = (jnp.zeros((2 * NARROW, 128), jnp.float32),) * 2
    sums = add(turned[me], sums)

    def came(round_, step):
        over = (step + round_) % 8
        return device(me, 8 - STEPS[step], (4 - over % 4) % 4 + 4 * (over // 4))

    def take(round_, sums, steps):
        for step in steps:
            sums = add(landed[came(round_, step)], sums)
        return sums

    for round_ in range(8):
        count = 7 if round_ == 1 else 8
        pltpu.make_async_copy(
            landed.at[pl.ds(0, count)], landed.at[pl.ds(0, count)], recv_sem.at[round_]
        ).wait()
        sums = take(round_, sums, range(count))

    low = jnp.sum(sums[0], axis=1, keepdims=True) * (1.0 / (N * ROWS))
    high = jnp.sum(sums[1], axis=1, keepdims=True) * (1.0 / (N * ROWS))
    scale = 1.0 / (high - low + 0.1)

    def finish(i, carry):
        block = (landed[i] - low) * scale
        rows = pl.ds(pl.multiple_of(i * ROWS, ROWS), ROWS)
        first_out[:, rows] = block[:NARROW]
        second_out[:, rows] = block[NARROW:]
        return carry

    lax.fori_loop(0, N, finish, 0, unroll=4)
    pltpu.make_async_copy(
        landed.at[pl.ds(0, N - 1)], landed.at[pl.ds(0, N - 1)], send_sem
    ).wait()


def shards(samples_in, second_samples_in):
    out = pltpu.VMEM((NARROW, N * ROWS), jnp.float32)
    first, second = pl.pallas_call(
        kernel,
        out_shape=(out, out),
        in_specs=[pl.BlockSpec(memory_space=pltpu.HBM)] * 2,
        out_specs=(pl.BlockSpec(memory_space=pltpu.VMEM),) * 2,
        scratch_shapes=[
            pltpu.VMEM((2, ROWS, WIDE), jnp.float32),
            pltpu.VMEM((N, 2 * NARROW, ROWS), jnp.float32),
            pltpu.VMEM((N, 2 * NARROW, ROWS), jnp.float32),
            pltpu.SemaphoreType.DMA((2, 8)),
            pltpu.SemaphoreType.DMA,
            pltpu.SemaphoreType.DMA((8,)),
        ],
        compiler_params=pltpu.CompilerParams(
            collective_id=0, has_side_effects=True, vmem_limit_bytes=59 * 2**20
        ),
    )(samples_in, second_samples_in)
    return first.T, second.T


def solution(mesh):
    placed = (P("batch", "group"), P("batch", "group"))
    return jax.shard_map(
        shards,
        mesh=mesh,
        in_specs=placed,
        out_specs=(P(None, ("group", "batch")), P(None, ("group", "batch"))),
        check_vma=False,
    )
```

time: 132 us -> 108 us (0.82)
  Pallas kernels: 0 us -> 105 us
  waiting for transfers between devices: 95.7 us -> 0 us
  starting transfers between devices: 20.6 us -> 0 us
  local copies, waits for them, and re-layouts: 9.08 us -> 2.64 us
  other arithmetic: 5.11 us -> 0 us
    pallas_call x0 -> x1, Pallas kernels: none -> 105 us  [shards(): pl.pallas_call(kernel, out_shape=(out, out), in_specs=[pl.BlockSpec(memor...]
    all_to_all x2 -> x0, waiting for transfers between devices: 95.7 us -> none  [the longest x1 48.7 us: shards(): lax.all_to_all(second_samples_in, 'batch', split_axis=1, concat_axis=0, t...]
    all_to_all x2 -> x0, starting transfers between devices: 20.6 us -> none  [the longest x1 13.2 us: shards(): lax.all_to_all(samples_in, 'batch', split_axis=1, concat_axis=0, tiled=True)]
    all_to_all x2 -> x0, local copies, waits for them, and re-layouts: 3.3 us -> none  [the longest x1 1.78 us: shards(): lax.all_to_all(second_samples_in, 'batch', split_axis=1, concat_axis=0, t...]
    unnamed x4 -> x2, local copies, waits for them, and re-layouts: 5.78 us -> 2.64 us
    reduce_sum x2 -> x0, other arithmetic: 2.61 us -> none  [the longest x1 2.14 us: shards(): jnp.mean(jnp.minimum(wide_second_standard, 1.0), axis=0)]
    div x3 -> x0, other arithmetic: 2.51 us -> none  [the longest x1 2.49 us: shards(): (wide_second_standard - low_second_standard) / (high_second_standard - lo...]
  transfers between devices with their start and end apart: 2 -> 0, of which waited for: 2 -> 0; matrix products, arithmetic and copies ran while one was open for 3% -> 0% of each run, Pallas kernels for 0% -> 0%
where the time goes in v1:
time: 108 us
  Pallas kernels  105 us (97%)
  local copies, waits for them, and re-layouts  2.64 us (2%)
    pallas_call x1, Pallas kernels, shards(): pl.pallas_call(kernel, out_shape=(out, out), in_specs=[pl.BlockSpec(memor...  105 us
    unnamed x2, local copies, waits for them, and re-layouts  2.64 us

profile of v1, /device:TPU:1, one launch (start us, length us, event | category | flops | bytes accessed | tf_op | source)
XLA Modules:
  0.0 108.3 jit_solution(8677786411748445043)
XLA Ops:
  0.6 105.0 %shard_map.41 = (f32[32,16384]{1,0:T(8,128)S(1)}, f32[32,16384]{1,0:T(8,128)S(1)}) custom-call(f32[256,2048]{1,0:T(8,128)} %a_ref.1, f32[256,2048]{1,0:T(8,128)} %b_ref.1), custom_call_target="tpu_custom_call" | custom-call | tf_op jit(solution)/shard_map/pallas_call | solution.py:130
  105.6 1.3 %copy.6 = f32[16384,32]{0,1:T(8,128)} copy(f32[16384,32]{0,1:T(8,128)S(1)} %bitcast.3) | data formatting | bytes 4194304
  107.0 1.3 %copy.7 = f32[16384,32]{0,1:T(8,128)} copy(f32[16384,32]{0,1:T(8,128)S(1)} %bitcast.2) | data formatting | bytes 4194304

commit v2 on v0

v2 whole, which is shorter than its diff:
```python
import jax
import jax.numpy as jnp
from jax import lax
from jax.experimental import pallas as pl
from jax.experimental.pallas import tpu as pltpu
from jax.sharding import PartitionSpec as P

MESH = pl.DeviceIdType.MESH
N = 64
ROWS, WIDE, NARROW = 256, 2048, 32
STEPS = (1, 7, 2, 6, 3, 5, 4, 0)
PAIR = 4 * NARROW


def kernel(
    a_ref, b_ref, landed, stats, held, turned, in_sem, send_sem, recv_sem, below, above, left, right
):
    me = lax.axis_index("batch")
    z, y, c = me // 8, (me // 2) % 4, me % 2

    def device(dz, dy, dc):
        return ((z + dz) % 8) * 8 + ((y + dy) % 4) * 2 + (c + dc) % 2

    def tell(sem, *offset):
        pl.semaphore_signal(
            sem, inc=1, device_id={"batch": device(*offset)}, device_id_type=MESH
        )

    barrier = pltpu.get_barrier_semaphore()
    neighbours = (
        (1, 0, 0), (1, 0, 1), (7, 0, 0), (7, 0, 1), (0, 0, 1), (0, 1, 0), (0, 3, 0)
    )
    for offset in neighbours:
        tell(barrier, *offset)

    def first_device(step, other):
        return ((z + STEPS[step]) % 8) * 8 + ((y // 2 + other) % 2) * 4

    def load(which, step, other):
        columns = pl.ds(pl.multiple_of(first_device(step, other) * NARROW, PAIR), PAIR)
        source = (a_ref, b_ref)[which]
        return pltpu.make_async_copy(
            source.at[:, columns], held.at[which, :, columns], in_sem.at[which, other, step]
        )

    for other in range(2):
        for step in range(8):
            for which in range(2):
                load(which, step, other).start()

    def turn(step, other):
        first = first_device(step, other)
        columns = pl.ds(pl.multiple_of(first * NARROW, PAIR), PAIR)
        for which in range(2):
            load(which, step, other).wait()
            block = held[which, :, columns].T
            turned[pl.ds(first, 4), which * NARROW : (which + 1) * NARROW, :] = block.reshape(
                4, NARROW, ROWS
            )

    def send(dz, dy, dc, group):
        to = device(dz, dy, dc)
        pltpu.make_async_remote_copy(
            src_ref=turned.at[to],
            dst_ref=landed.at[me],
            send_sem=send_sem,
            recv_sem=recv_sem.at[group],
            device_id={"batch": to},
            device_id_type=MESH,
        ).start()

    def send_column(step):
        send(STEPS[step], 0, 0, 0)
        send(STEPS[step], 0, 1, 0)

    turn(0, 0)
    turn(1, 0)
    pl.semaphore_wait(barrier, len(neighbours))
    tell(below, 1, 0, 0)
    tell(above, 7, 0, 0)
    send_column(0)
    turn(2, 0)
    send_column(1)
    pl.semaphore_wait(below, 1)
    tell(below, 1, 0, 0)
    pl.semaphore_wait(above, 1)
    tell(above, 7, 0, 0)
    turn(3, 0)
    send_column(2)
    turn(4, 0)
    send_column(3)
    pl.semaphore_wait(below, 1)
    tell(below, 1, 0, 0)
    pl.semaphore_wait(above, 1)
    turn(5, 0)
    send_column(4)
    turn(6, 0)
    send_column(5)
    pl.semaphore_wait(below, 1)
    tell(left, 0, 1, 0)
    tell(right, 0, 3, 0)
    turn(7, 0)
    send_column(6)
    turn(0, 1)
    send(0, 0, 1, 0)
    pl.semaphore_wait(left, 1)
    tell(left, 0, 1, 0)
    pl.semaphore_wait(right, 1)
    for step in range(1, 8):
        turn(step, 1)
    pl.semaphore_wait(left, 1)

    def over(round_, step):
        o = (step + round_) % 6
        return 1 + o % 3, o // 3

    def send_round(round_, carry):
        for step in range(8):
            dy, dc = over(round_, step)
            send(STEPS[step], dy, dc, 1 + round_)
        return carry

    lax.fori_loop(0, 6, send_round, 0)

    def add(block, sums):
        low, high = sums
        left, right = block[:, :128], block[:, 128:]
        low = low + (jnp.minimum(left, 1.0) + jnp.minimum(right, 1.0))
        high = high + (jnp.maximum(left, 1.0) + jnp.maximum(right, 1.0))
        return low, high

    def take(sums, dz, dy, dc):
        return add(landed[device(8 - dz, 4 - dy, dc)], sums)

    def wait(count, sem):
        pltpu.make_async_copy(landed.at[pl.ds(0, count)], landed.at[pl.ds(0, count)], sem).wait()

    landed[me] = turned[me]
    sums = (jnp.zeros((2 * NARROW, 128), jnp.float32),) * 2
    sums = add(turned[me], sums)
    wait(15, recv_sem.at[0])
    for dz in STEPS[:7]:
        for dc in range(2):
            sums = take(sums, dz, 0, dc)
    sums = take(sums, 0, 0, 1)

    def take_round(round_, sums):
        wait(8, recv_sem.at[1 + round_])
        for step in range(8):
            sums = take(sums, STEPS[step], *over(round_, step))
        return sums

    sums = lax.fori_loop(0, 6, take_round, sums)

    low = jnp.sum(sums[0], axis=1, keepdims=True) * (1.0 / (N * ROWS))
    high = jnp.sum(sums[1], axis=1, keepdims=True) * (1.0 / (N * ROWS))
    stats[0] = jnp.broadcast_to(low, stats.shape[1:])
    stats[1] = jnp.broadcast_to(1.0 / (high - low + 0.1), stats.shape[1:])
    wait(N - 1, send_sem)


def write(landed, stats, first_out, second_out, ready, sem):
    pieces = sem.shape[1]
    each = N // pieces

    def put(which, piece):
        out = (first_out, second_out)[which]
        rows = pl.ds(pl.multiple_of(piece * each * ROWS, each * ROWS), each * ROWS)
        return pltpu.make_async_copy(ready.at[which, :, rows], out.at[:, rows], sem.at[which, piece])

    low, factor = stats[0, :, :1], stats[1, :, :1]

    def finish(piece, carry):
        for i in range(each):
            block = (landed[piece * each + i] - low) * factor
            rows = pl.ds(pl.multiple_of((piece * each + i) * ROWS, ROWS), ROWS)
            ready[0, :, rows] = block[:NARROW]
            ready[1, :, rows] = block[NARROW:]
        put(0, piece).start()
        put(1, piece).start()
        return carry

    lax.fori_loop(0, pieces, finish, 0)

    def drain(piece, carry):
        put(0, piece).wait()
        put(1, piece).wait()
        return carry

    lax.fori_loop(0, pieces, drain, 0)


def shards(samples_in, second_samples_in):
    whole = pltpu.VMEM((N, 2 * NARROW, ROWS), jnp.float32)
    columns = pltpu.VMEM((2, 2 * NARROW, 128), jnp.float32)
    vmem, hbm = pl.BlockSpec(memory_space=pltpu.VMEM), pl.BlockSpec(memory_space=pltpu.HBM)
    landed, stats = pl.pallas_call(
        kernel,
        out_shape=(whole, columns),
        in_specs=[hbm] * 2,
        out_specs=(vmem,) * 2,
        scratch_shapes=[
            pltpu.VMEM((2, ROWS, WIDE), jnp.float32),
            whole,
            pltpu.SemaphoreType.DMA((2, 2, 8)),
            pltpu.SemaphoreType.DMA,
            pltpu.SemaphoreType.DMA((7,)),
            pltpu.SemaphoreType.REGULAR,
            pltpu.SemaphoreType.REGULAR,
            pltpu.SemaphoreType.REGULAR,
            pltpu.SemaphoreType.REGULAR,
        ],
        compiler_params=pltpu.CompilerParams(
            collective_id=0, has_side_effects=True, vmem_limit_bytes=58 * 2**20
        ),
    )(samples_in, second_samples_in)
    out = jax.ShapeDtypeStruct((NARROW, N * ROWS), jnp.float32)
    first, second = pl.pallas_call(
        write,
        out_shape=(out, out),
        in_specs=[vmem] * 2,
        out_specs=(hbm,) * 2,
        scratch_shapes=[
            pltpu.VMEM((2, NARROW, N * ROWS), jnp.float32),
            pltpu.SemaphoreType.DMA((2, 8)),
        ],
        compiler_params=pltpu.CompilerParams(vmem_limit_bytes=16 * 2**20),
    )(landed, stats)
    return first.T, second.T


def solution(mesh):
    placed = (P("batch", "group"), P("batch", "group"))
    return jax.shard_map(
        shards,
        mesh=mesh,
        in_specs=placed,
        out_specs=(P(None, ("group", "batch")), P(None, ("group", "batch"))),
        check_vma=False,
    )
```

time: 132 us -> 105 us (0.80)
  Pallas kernels: 0 us -> 104 us
  waiting for transfers between devices: 95.7 us -> 0 us
  starting transfers between devices: 20.6 us -> 0 us
  local copies, waits for them, and re-layouts: 9.08 us -> 0 us
  other arithmetic: 5.11 us -> 0 us
    pallas_call x0 -> x2, Pallas kernels: none -> 104 us  [the longest x1 102 us: shards(): pl.pallas_call(kernel, out_shape=(whole, columns), in_specs=[hbm] * 2, ou...]
    all_to_all x2 -> x0, waiting for transfers between devices: 95.7 us -> none  [the longest x1 48.7 us: shards(): lax.all_to_all(second_samples_in, 'batch', split_axis=1, concat_axis=0, t...]
    all_to_all x2 -> x0, starting transfers between devices: 20.6 us -> none  [the longest x1 13.2 us: shards(): lax.all_to_all(samples_in, 'batch', split_axis=1, concat_axis=0, tiled=True)]
    unnamed x4 -> x0, local copies, waits for them, and re-layouts: 5.78 us -> none
    all_to_all x2 -> x0, local copies, waits for them, and re-layouts: 3.3 us -> none  [the longest x1 1.78 us: shards(): lax.all_to_all(second_samples_in, 'batch', split_axis=1, concat_axis=0, t...]
    reduce_sum x2 -> x0, other arithmetic: 2.61 us -> none  [the longest x1 2.14 us: shards(): jnp.mean(jnp.minimum(wide_second_standard, 1.0), axis=0)]
    div x3 -> x0, other arithmetic: 2.51 us -> none  [the longest x1 2.49 us: shards(): (wide_second_standard - low_second_standard) / (high_second_standard - lo...]
  transfers between devices with their start and end apart: 2 -> 0, of which waited for: 2 -> 0; matrix products, arithmetic and copies ran while one was open for 3% -> 0% of each run, Pallas kernels for 0% -> 0%
where the time goes in v2:
time: 105 us
  Pallas kernels  104 us (99%)
    pallas_call x1, Pallas kernels, shards(): pl.pallas_call(kernel, out_shape=(whole, columns), in_specs=[hbm] * 2, ou...  102 us
    pallas_call x1, Pallas kernels, shards(): pl.pallas_call(write, out_shape=(out, out), in_specs=[vmem] * 2, out_spec...  2.28 us

profile of v2, /device:TPU:1, one launch (start us, length us, event | category | flops | bytes accessed | tf_op | source)
XLA Modules:
  0.0 105.1 jit_solution(17779425895848120939)
XLA Ops:
  0.6 102.2 %shard_map.41 = (f32[64,64,256]{2,1,0:T(8,128)S(1)}, f32[2,64,128]{2,1,0:T(8,128)S(1)}) custom-call(f32[256,2048]{1,0:T(8,128)} %a_ref.1, f32[256,2048]{1,0:T(8,128)} %b_ref.1), custom_call_target="tpu_custom_call" | custom-call | tf_op jit(solution)/shard_map/pallas_call | solution.py:197
  102.8 2.3 %shard_map.42 = (f32[32,16384]{1,0:T(8,128)}, f32[32,16384]{1,0:T(8,128)}) custom-call(f32[64,64,256]{2,1,0:T(8,128)S(1)} %get-tuple-element.6.landed, f32[2,64,128]{2,1,0:T(8,128)S(1)} %get-tuple-element.7.stats), custom_call_target="tpu_custom_call" | custom-call | tf_op jit(solution)/shard_map/pallas_call | solution.py:218

commit v3 on v2

--- a/solution.py
+++ b/solution.py
@@ -110,17 +110,25 @@
         turn(step, 1)
     pl.semaphore_wait(left, 1)
 
-    def over(round_, step):
-        o = (step + round_) % 6
-        return 1 + o % 3, o // 3
-
-    def send_round(round_, carry):
-        for step in range(8):
-            dy, dc = over(round_, step)
-            send(STEPS[step], dy, dc, 1 + round_)
-        return carry
-
-    lax.fori_loop(0, 6, send_round, 0)
+    def over(round_, dz):
+        m = (dz + 7) % 8
+        o = (2 * m + (m // 4) * (13 - 4 * m) + 6 + round_) % 6
+        return 1 + o // 2, o % 2
+
+    def send_step(round_, dz):
+        dy, dc = over(round_, dz)
+        send(dz, dy, dc, 1 + round_)
+
+    def to_half(q, half, k):
+        send_step(q, (half * 4 + (z + k) % 4 + 8 - z) % 8)
+
+    for q in range(4):
+        for dz in STEPS:
+            send_step(q, dz)
+    for q in (4, 5):
+        for half in range(2):
+            for k in range(4):
+                to_half(q, half, k)
 
     def add(block, sums):
         low, high = sums
@@ -147,7 +155,7 @@
     def take_round(round_, sums):
         wait(8, recv_sem.at[1 + round_])
         for step in range(8):
-            sums = take(sums, STEPS[step], *over(round_, step))
+            sums = take(sums, STEPS[step], *over(round_, STEPS[step]))
         return sums
 
     sums = lax.fori_loop(0, 6, take_round, sums)

time: 105 us -> 103 us (0.981)
  the two profiles are of different devices: /device:TPU:1 before, /device:TPU:32 now
where the time goes in v3:
time: 103 us
  Pallas kernels  102 us (99%)
    pallas_call x1, Pallas kernels, shards(): pl.pallas_call(kernel, out_shape=(whole, columns), in_specs=[hbm] * 2, ou...  100 us
    pallas_call x1, Pallas kernels, shards(): pl.pallas_call(write, out_shape=(out, out), in_specs=[vmem] * 2, out_spec...  2.28 us

profile of v3, /device:TPU:32, one launch (start us, length us, event | category | flops | bytes accessed | tf_op | source)
XLA Modules:
  0.0 103.1 jit_solution(1206025975005624674)
XLA Ops:
  0.6 100.2 %shard_map.41 = (f32[64,64,256]{2,1,0:T(8,128)S(1)}, f32[2,64,128]{2,1,0:T(8,128)S(1)}) custom-call(f32[256,2048]{1,0:T(8,128)} %a_ref.1, f32[256,2048]{1,0:T(8,128)} %b_ref.1), custom_call_target="tpu_custom_call" | custom-call | tf_op jit(solution)/shard_map/pallas_call | solution.py:205
  100.8 2.3 %shard_map.42 = (f32[32,16384]{1,0:T(8,128)}, f32[32,16384]{1,0:T(8,128)}) custom-call(f32[64,64,256]{2,1,0:T(8,128)S(1)} %get-tuple-element.6.landed, f32[2,64,128]{2,1,0:T(8,128)S(1)} %get-tuple-element.7.stats), custom_call_target="tpu_custom_call" | custom-call | tf_op jit(solution)/shard_map/pallas_call | solution.py:226

commit v4 on v3

--- a/solution.py
+++ b/solution.py
@@ -33,8 +33,13 @@
     for offset in neighbours:
         tell(barrier, *offset)
 
+    sign = z // 2 % 2 * 2 - 1
+
+    def turned_at(step):
+        return (8 + sign * STEPS[step]) % 8
+
     def first_device(step, other):
-        return ((z + STEPS[step]) % 8) * 8 + ((y // 2 + other) % 2) * 4
+        return ((z + turned_at(step)) % 8) * 8 + ((y // 2 + other) % 2) * 4
 
     def load(which, step, other):
         columns = pl.ds(pl.multiple_of(first_device(step, other) * NARROW, PAIR), PAIR)
@@ -70,32 +75,32 @@
         ).start()
 
     def send_column(step):
-        send(STEPS[step], 0, 0, 0)
-        send(STEPS[step], 0, 1, 0)
+        send(turned_at(step), 0, 0, 0)
+        send(turned_at(step), 0, 1, 0)
 
     turn(0, 0)
-    turn(1, 0)
     pl.semaphore_wait(barrier, len(neighbours))
     tell(below, 1, 0, 0)
     tell(above, 7, 0, 0)
     send_column(0)
+    turn(1, 0)
+    send_column(1)
     turn(2, 0)
-    send_column(1)
     pl.semaphore_wait(below, 1)
     tell(below, 1, 0, 0)
     pl.semaphore_wait(above, 1)
     tell(above, 7, 0, 0)
+    send_column(2)
     turn(3, 0)
-    send_column(2)
+    send_column(3)
     turn(4, 0)
-    send_column(3)
     pl.semaphore_wait(below, 1)
     tell(below, 1, 0, 0)
     pl.semaphore_wait(above, 1)
+    send_column(4)
     turn(5, 0)
-    send_column(4)
+    send_column(5)
     turn(6, 0)
-    send_column(5)
     pl.semaphore_wait(below, 1)
     tell(left, 0, 1, 0)
     tell(right, 0, 3, 0)
@@ -123,8 +128,8 @@
         send_step(q, (half * 4 + (z + k) % 4 + 8 - z) % 8)
 
     for q in range(4):
-        for dz in STEPS:
-            send_step(q, dz)
+        for step in range(8):
+            send_step(q, turned_at(step))
     for q in (4, 5):
         for half in range(2):
             for k in range(4):

time: 103 us -> 103 us (level)
  the two profiles are of different devices: /device:TPU:32 before, /device:TPU:1 now
where the time goes in v4:
time: 103 us
  Pallas kernels  102 us (99%)
    pallas_call x1, Pallas kernels, shards(): pl.pallas_call(kernel, out_shape=(whole, columns), in_specs=[hbm] * 2, ou...  99.9 us
    pallas_call x1, Pallas kernels, shards(): pl.pallas_call(write, out_shape=(out, out), in_specs=[vmem] * 2, out_spec...  2.28 us

profile of v4, /device:TPU:1, one launch (start us, length us, event | category | flops | bytes accessed | tf_op | source)
XLA Modules:
  0.0 102.8 jit_solution(12628402204738058351)
XLA Ops:
  0.6 99.9 %shard_map.41 = (f32[64,64,256]{2,1,0:T(8,128)S(1)}, f32[2,64,128]{2,1,0:T(8,128)S(1)}) custom-call(f32[256,2048]{1,0:T(8,128)} %a_ref.1, f32[256,2048]{1,0:T(8,128)} %b_ref.1), custom_call_target="tpu_custom_call" | custom-call | tf_op jit(solution)/shard_map/pallas_call | solution.py:210
  100.5 2.3 %shard_map.42 = (f32[32,16384]{1,0:T(8,128)}, f32[32,16384]{1,0:T(8,128)}) custom-call(f32[64,64,256]{2,1,0:T(8,128)S(1)} %get-tuple-element.6.landed, f32[2,64,128]{2,1,0:T(8,128)S(1)} %get-tuple-element.7.stats), custom_call_target="tpu_custom_call" | custom-call | tf_op jit(solution)/shard_map/pallas_call | solution.py:231

commit v5 on v4

--- a/solution.py
+++ b/solution.py
@@ -181,14 +181,15 @@
         rows = pl.ds(pl.multiple_of(piece * each * ROWS, each * ROWS), each * ROWS)
         return pltpu.make_async_copy(ready.at[which, :, rows], out.at[:, rows], sem.at[which, piece])
 
-    low, factor = stats[0, :, :1], stats[1, :, :1]
+    low, factor = stats[0], stats[1]
 
     def finish(piece, carry):
         for i in range(each):
-            block = (landed[piece * each + i] - low) * factor
-            rows = pl.ds(pl.multiple_of((piece * each + i) * ROWS, ROWS), ROWS)
-            ready[0, :, rows] = block[:NARROW]
-            ready[1, :, rows] = block[NARROW:]
+            for side in range(0, ROWS, 128):
+                block = (landed[piece * each + i, :, side : side + 128] - low) * factor
+                rows = pl.ds(pl.multiple_of((piece * each + i) * ROWS + side, 128), 128)
+                ready[0, :, rows] = block[:NARROW]
+                ready[1, :, rows] = block[NARROW:]
         put(0, piece).start()
         put(1, piece).start()
         return carry

time: 103 us -> 103 us (level)
  no operation moved by 1% of the time
where the time goes in v5:
time: 103 us
  Pallas kernels  102 us (99%)
    pallas_call x1, Pallas kernels, shards(): pl.pallas_call(kernel, out_shape=(whole, columns), in_specs=[hbm] * 2, ou...  99.9 us
    pallas_call x1, Pallas kernels, shards(): pl.pallas_call(write, out_shape=(out, out), in_specs=[vmem] * 2, out_spec...  2.19 us

profile of v5, /device:TPU:1, one launch (start us, length us, event | category | flops | bytes accessed | tf_op | source)
XLA Modules:
  0.0 102.7 jit_solution(18129770098261186249)
XLA Ops:
  0.6 99.9 %shard_map.41 = (f32[64,64,256]{2,1,0:T(8,128)S(1)}, f32[2,64,128]{2,1,0:T(8,128)S(1)}) custom-call(f32[256,2048]{1,0:T(8,128)} %a_ref.1, f32[256,2048]{1,0:T(8,128)} %b_ref.1), custom_call_target="tpu_custom_call" | custom-call | tf_op jit(solution)/shard_map/pallas_call | solution.py:211
  100.5 2.2 %shard_map.42 = (f32[32,16384]{1,0:T(8,128)}, f32[32,16384]{1,0:T(8,128)}) custom-call(f32[64,64,256]{2,1,0:T(8,128)S(1)} %get-tuple-element.6.landed, f32[2,64,128]{2,1,0:T(8,128)S(1)} %get-tuple-element.7.stats), custom_call_target="tpu_custom_call" | custom-call | tf_op jit(solution)/shard_map/pallas_call | solution.py:232

commit v6 on v5

--- a/solution.py
+++ b/solution.py
@@ -117,7 +117,7 @@
 
     def over(round_, dz):
         m = (dz + 7) % 8
-        o = (2 * m + (m // 4) * (13 - 4 * m) + 6 + round_) % 6
+        o = (2 * m + (m // 4) * (13 - 4 * m) + 6 + 5 * round_) % 6
         return 1 + o // 2, o % 2
 
     def send_step(round_, dz):
@@ -128,8 +128,8 @@
         send_step(q, (half * 4 + (z + k) % 4 + 8 - z) % 8)
 
     for q in range(4):
-        for step in range(8):
-            send_step(q, turned_at(step))
+        for dz in STEPS:
+            send_step(q, dz)
     for q in (4, 5):
         for half in range(2):
             for k in range(4):

time: 103 us -> 102 us (level)
  no operation moved by 1% of the time
where the time goes in v6:
time: 102 us
  Pallas kernels  101 us (99%)
    pallas_call x1, Pallas kernels, shards(): pl.pallas_call(kernel, out_shape=(whole, columns), in_specs=[hbm] * 2, ou...  99.1 us
    pallas_call x1, Pallas kernels, shards(): pl.pallas_call(write, out_shape=(out, out), in_specs=[vmem] * 2, out_spec...  2.19 us

profile of v6, /device:TPU:1, one launch (start us, length us, event | category | flops | bytes accessed | tf_op | source)
XLA Modules:
  0.0 101.9 jit_solution(12834419192833492630)
XLA Ops:
  0.6 99.1 %shard_map.41 = (f32[64,64,256]{2,1,0:T(8,128)S(1)}, f32[2,64,128]{2,1,0:T(8,128)S(1)}) custom-call(f32[256,2048]{1,0:T(8,128)} %a_ref.1, f32[256,2048]{1,0:T(8,128)} %b_ref.1), custom_call_target="tpu_custom_call" | custom-call | tf_op jit(solution)/shard_map/pallas_call | solution.py:211
  99.7 2.2 %shard_map.42 = (f32[32,16384]{1,0:T(8,128)}, f32[32,16384]{1,0:T(8,128)}) custom-call(f32[64,64,256]{2,1,0:T(8,128)S(1)} %get-tuple-element.6.landed, f32[2,64,128]{2,1,0:T(8,128)S(1)} %get-tuple-element.7.stats), custom_call_target="tpu_custom_call" | custom-call | tf_op jit(solution)/shard_map/pallas_call | solution.py:232

commit v7 on v6

--- a/solution.py
+++ b/solution.py
@@ -28,7 +28,7 @@
 
     barrier = pltpu.get_barrier_semaphore()
     neighbours = (
-        (1, 0, 0), (1, 0, 1), (7, 0, 0), (7, 0, 1), (0, 0, 1), (0, 1, 0), (0, 3, 0)
+        (0, 1, 0), (0, 3, 0), (1, 0, 0), (7, 0, 0), (1, 0, 1), (7, 0, 1), (0, 0, 1)
     )
     for offset in neighbours:
         tell(barrier, *offset)

time: 102 us -> 103 us (level)
  no operation moved by 1% of the time
where the time goes in v7:
time: 103 us
  Pallas kernels  102 us (99%)
    pallas_call x1, Pallas kernels, shards(): pl.pallas_call(kernel, out_shape=(whole, columns), in_specs=[hbm] * 2, ou...  100 us
    pallas_call x1, Pallas kernels, shards(): pl.pallas_call(write, out_shape=(out, out), in_specs=[vmem] * 2, out_spec...  2.19 us

profile of v7, /device:TPU:1, one launch (start us, length us, event | category | flops | bytes accessed | tf_op | source)
XLA Modules:
  0.0 102.9 jit_solution(4014738328037533709)
XLA Ops:
  0.6 100.1 %shard_map.41 = (f32[64,64,256]{2,1,0:T(8,128)S(1)}, f32[2,64,128]{2,1,0:T(8,128)S(1)}) custom-call(f32[256,2048]{1,0:T(8,128)} %a_ref.1, f32[256,2048]{1,0:T(8,128)} %b_ref.1), custom_call_target="tpu_custom_call" | custom-call | tf_op jit(solution)/shard_map/pallas_call | solution.py:211
  100.7 2.2 %shard_map.42 = (f32[32,16384]{1,0:T(8,128)}, f32[32,16384]{1,0:T(8,128)}) custom-call(f32[64,64,256]{2,1,0:T(8,128)S(1)} %get-tuple-element.6.landed, f32[2,64,128]{2,1,0:T(8,128)S(1)} %get-tuple-element.7.stats), custom_call_target="tpu_custom_call" | custom-call | tf_op jit(solution)/shard_map/pallas_call | solution.py:232
